TPU v7x, 32 devices: a whole 2x2x4 slice. The times are simulated.
32 devices in a mesh: group: 4 (over z), batch: 8 (over y, x, core).
Axes of the slice: x: 2, y: 2, z: 4, core: 2. Of those that a mesh axis runs over, the one named last changes fastest.
Arguments:
- embeds: bfloat16 [65536, 256], P(('group', 'batch')), may hold values from -6 to 6
- out_grad: bfloat16 [65536, 256], P(('group', 'batch')), may hold values from -48 to 48
- w_query: bfloat16 [256, 256], replicated, may hold values from -0.375 to 0.375
- w_key: bfloat16 [256, 256], replicated, may hold values from -0.375 to 0.375
- w_value: bfloat16 [256, 256], replicated, may hold values from -0.375 to 0.375
- lengths: int32 [128], P(('group', 'batch')), may hold values from 1 to 512, as said below
- item_rows: int32 [65536], P(('group', 'batch')), may hold values from 0 to 2047, as said below
- tile_owner: int32 [512], P(('group', 'batch')), may hold values from 0 to 3, as said below
Outputs:
- table_grad: float32 [8192, 256], P(('group', 'batch'))
Inputs may be any that keep to these rules, and one draw needn't show every extreme that they name: `lengths`: a history's live tokens are its first positions; in every draw some history has exactly 512 live tokens. `tile_owner`: among the first 8 tiles of each device's own tiles, and among the last 8, every group owns exactly 2 tiles. `item_rows`: of the 128 tokens of each tile, at most 32 have rows r with the same r // 256, and in every tile some value of r // 256 is taken by exactly 32 tokens.
All inputs are finite; a program needn't handle non-finite values.
Results may differ from a plain program's by a relative error of at most 0.0024.
The roundings to bfloat16 on the way count: a program that leaves them out, or rounds other values in their place, can miss the bound.
Values may be sent and summed in bfloat16 or wider, within the bound.
No kernel may reach another device: no remote copies, remote signals or barrier semaphores. Data moves between devices by JAX's collectives and lax.ppermute only.
A program may use at most 64 MiB of HBM per device.

v0:
```python
import math
import jax
import jax.numpy as jnp
from jax import lax
from jax.sharding import PartitionSpec as P

HEADS = 2
TILE = 128
SEQ_LEN = 512
ROWS_DEV = 256


def sequence_grads(query, key_rows, value, grad_out, count, w_query, w_key, w_value):
    span = query.shape[0]
    position = lax.broadcasted_iota(jnp.int32, (span, span), 0)
    other = lax.broadcasted_iota(jnp.int32, (span, span), 1)
    live = ((other <= position) & (position < count)).astype(jnp.float32)
    weight = live / count.astype(jnp.float32)
    scale = 1.0 / math.sqrt(query.shape[2])
    scores = jnp.einsum("ihd,jhd->hij", query, key_rows, preferred_element_type=jnp.float32) * scale
    sigma = jax.nn.sigmoid(scores)
    attend = (scores * sigma * weight).astype(jnp.bfloat16)
    value_grad = jnp.einsum(
        "hij,ihd->jhd", attend, grad_out, preferred_element_type=jnp.float32
    ).astype(jnp.bfloat16)
    attend_grad = jnp.einsum("ihd,jhd->hij", grad_out, value, preferred_element_type=jnp.float32)
    score_grad = (attend_grad * weight * sigma * (1.0 + scores * (1.0 - sigma))).astype(
        jnp.bfloat16
    )
    query_grad = (
        jnp.einsum("hij,jhd->ihd", score_grad, key_rows, preferred_element_type=jnp.float32) * scale
    ).astype(jnp.bfloat16)
    key_grad = (
        jnp.einsum("hij,ihd->jhd", score_grad, query, preferred_element_type=jnp.float32) * scale
    ).astype(jnp.bfloat16)
    width = w_query.shape[0]
    token = jnp.dot(query_grad.reshape(span, width), w_query.T, preferred_element_type=jnp.float32)
    token = token + jnp.dot(
        key_grad.reshape(span, width), w_key.T, preferred_element_type=jnp.float32
    )
    token = token + jnp.dot(
        value_grad.reshape(span, width), w_value.T, preferred_element_type=jnp.float32
    )
    return token.astype(jnp.bfloat16)


def token_grads(embeds, out_grad, w_query, w_key, w_value, lengths):
    history_count = lengths.shape[0]
    width = embeds.shape[1]
    head_size = width // HEADS

    def project(weight_matrix):
        return (
            jnp.dot(embeds, weight_matrix, preferred_element_type=jnp.float32)
            .astype(jnp.bfloat16)
            .reshape(history_count, SEQ_LEN, HEADS, head_size)
        )

    query = project(w_query)
    key_rows = project(w_key)
    value = project(w_value)
    grad_heads = out_grad.reshape(history_count, SEQ_LEN, HEADS, head_size)
    half_span = SEQ_LEN // 2

    def short_history(item):
        front = sequence_grads(
            item[0][:half_span],
            item[1][:half_span],
            item[2][:half_span],
            item[3][:half_span],
            item[4],
            w_query,
            w_key,
            w_value,
        )
        return jnp.concatenate(
            [front, jnp.zeros((SEQ_LEN - half_span, width), jnp.bfloat16)], axis=0
        )

    def whole_history(item):
        return sequence_grads(item[0], item[1], item[2], item[3], item[4], w_query, w_key, w_value)

    def one_history(item):
        return lax.cond(item[4] <= half_span, short_history, whole_history, item)

    result = lax.map(one_history, (query, key_rows, value, grad_heads, lengths))
    return result.reshape(history_count * SEQ_LEN, width)


def onehot_sum(row_count, tile_values, tile_rows, block_rows, initial):
    width = tile_values.shape[-1]
    flat_values = tile_values.reshape(-1, width)
    flat_rows = tile_rows.reshape(-1)
    step_count = flat_rows.shape[0] // block_rows
    target = lax.broadcasted_iota(jnp.int32, (row_count, 1), 0)

    def add_block(accum, item):
        onehot = (target == item[1][None, :]).astype(jnp.bfloat16)
        return (accum + jnp.dot(onehot, item[0], preferred_element_type=jnp.float32), None)

    blocks = (
        flat_values.reshape(step_count, block_rows, width),
        flat_rows.reshape(step_count, block_rows),
    )
    accum, unused = lax.scan(add_block, initial, blocks)
    return accum


def on_device(embeds, out_grad, w_query, w_key, w_value, lengths, item_rows, tile_owner):
    live_total = lax.psum(jnp.sum(lengths.astype(jnp.float32)), ("group", "batch"))
    device_count = lax.axis_size("group") * lax.axis_size("batch")
    scale_factor = embeds.shape[0] * device_count / live_total
    token_grad = token_grads(embeds, out_grad, w_query, w_key, w_value, lengths)
    width = token_grad.shape[1]
    ranking = jnp.argsort(tile_owner, stable=True)
    tile_values = token_grad.reshape(-1, TILE, width)[ranking]
    tile_rows = item_rows.reshape(-1, TILE)[ranking]
    got_values, got_rows = (
        lax.all_to_all(tile_values, "group", split_axis=0, concat_axis=0, tiled=True),
        lax.all_to_all(tile_rows, "group", split_axis=0, concat_axis=0, tiled=True),
    )
    empty_rows = jnp.zeros((ROWS_DEV * lax.axis_size("batch"), width), jnp.float32)
    table = lax.psum_scatter(
        onehot_sum(ROWS_DEV * lax.axis_size("batch"), got_values, got_rows, 4 * TILE, empty_rows),
        "batch",
        scatter_dimension=0,
        tiled=True,
    )
    return scale_factor * table


def solution(mesh):
    in_specs = (
        P(("group", "batch"), None),
        P(("group", "batch"), None),
        P(),
        P(),
        P(),
        P(("group", "batch")),
        P(("group", "batch")),
        P(("group", "batch")),
    )
    out_specs = P(("group", "batch"), None)
    return jax.shard_map(
        on_device, mesh=mesh, in_specs=in_specs, out_specs=out_specs, check_vma=False
    )
```

profile of v0, /device:TPU:0, one launch (start us, length us, event | category | flops | bytes accessed | tf_op | source)
XLA Modules:
  0.0 158.3 jit_solution(10579940593462021619)
XLA Ops:
  6.5 2.0 %sort.17 = (s32[16]{0:T(128)}, s32[16]{0:T(128)S(1)}) sort(s32[16]{0:T(128)} %param.21, s32[16]{0:T(128)S(1)} %iota.48), dimensions={0}, to_apply=%region_6.7 | sort | flops 64 | bytes 256 | tf_op jit(solution)/shard_map/jit(argsort)/sort | solution.py:115
  8.5 1.8 %gather_fusion = s32[16,128]{1,0:T(8,128)} fusion(s32[16,128]{1,0:T(8,128)} %bitcast.105, s32[1024]{0:T(1024)S(1)} %pad_clamp_fusion), kind=kCustom, calls=%fused_computation | custom fusion | bytes 16448 | tf_op jit(solution)/shard_map/gather | solution.py:117
  10.4 6.3 %all-to-all-start = ((s32[4,4,128]{2,1,0:T(4,128)}), s32[4,4,128]{2,1,0:T(4,128)S(1)}, u32[]{:S(2)}, u32[]{:S(2)}) async-start(s32[4,4,128]{2,1,0:T(4,128)} %bitcast.20), calls=%async_computation | async-start | bytes 16384 | tf_op jit(solution)/shard_map/all_to_all | solution.py:120
  16.7 2.2 %reshape.79 = bf16[4,512,2,128]{3,2,1,0:T(2,128)(2,1)} reshape(bf16[2048,256]{1,0:T(8,128)(2,1)} %param.15) | data formatting | bytes 2097152 | tf_op jit(solution)/shard_map/reshape | solution.py:62
  18.9 0.4 convolution_convert_fusion.4
  19.4 0.3 reshape.77
  19.8 0.4 convolution_convert_fusion.3
  20.3 1.1 reshape.78
  21.4 0.4 convolution_convert_fusion.2
  21.8 1.1 reshape.80
  23.0 34.3 %while.21 = (s32[]{:T(128)}, bf16[4,512,256]{2,1,0:T(8,128)(2,1)}, s32[4]{0:T(128)S(1)}, bf16[4,512,2,128]{3,2,1,0:T(2,128)(2,1)S(1)}, bf16[4,512,2,128]{3,2,1,0...) while((s32[]{:T(128)}, bf16[4,512,256]{2,1,0:T(8,128)(2,1)}, ...), condition=%wide.region_5.6_spmd, body=%wide.region_2.5_spmd.sunk | while | flops 883687936 | bytes 23463240 | solution.py:86
  23.0 0.6 dynamic_slice.43
  24.3 1.4 constant_dynamic-slice_fusion.8
  25.8 1.3 constant_dynamic-slice_fusion.9
  27.2 3.6 %conditional.2 = (bf16[1,512,256]{2,1,0:T(8,128)(2,1)S(1)}) conditional(s32[]{:T(128)} %convert_element_type.105, (bf16[512,2,128]{2,0,1:T(8,128)(2,1)S(1)}, bf16[512,2,128]{2,0,1:T(8,128)(2,1)S(1)}, s32[]{:T(128)}, bf16[512,2,128]{2,0,1:T(8,128)(2,1)S(1)}, bf16[512,2,128]{2,0,1:T(8,128)(2,1)S(1)}, /*index=5*/bf16[256,256]{1,0:T(8,128)(2,1)S(1)}, ...), branch_computations={%region_3.3_spmd, %region_4.4_spmd} | conditional | flops 883687936 | bytes 18744356 | solution.py:84
  28.0 0.7 iota_compare_fusion.3
  29.0 0.3 fusion.12
  29.3 0.3 convolution_convert_fusion.1
  29.9 0.2 fusion.13
  30.3 0.2 convolution_add_fusion.3
  30.8 0.7 constant_dynamic-update-slice_fusion.2
  31.6 0.6 dynamic_slice.43
  32.9 1.4 constant_dynamic-slice_fusion.8
  34.4 1.3 constant_dynamic-slice_fusion.9
  35.8 3.6 %conditional.2 = (bf16[1,512,256]{2,1,0:T(8,128)(2,1)S(1)}) conditional(s32[]{:T(128)} %convert_element_type.105, (bf16[512,2,128]{2,0,1:T(8,128)(2,1)S(1)}, bf16[512,2,128]{2,0,1:T(8,128)(2,1)S(1)}, s32[]{:T(128)}, bf16[512,2,128]{2,0,1:T(8,128)(2,1)S(1)}, bf16[512,2,128]{2,0,1:T(8,128)(2,1)S(1)}, /*index=5*/bf16[256,256]{1,0:T(8,128)(2,1)S(1)}, ...), branch_computations={%region_3.3_spmd, %region_4.4_spmd} | conditional | flops 883687936 | bytes 18744356 | solution.py:84
  36.5 0.7 iota_compare_fusion.3
  37.6 0.3 fusion.12
  37.9 0.3 convolution_convert_fusion.1
  38.4 0.2 fusion.13
  38.9 0.2 convolution_add_fusion.3
  39.4 0.7 constant_dynamic-update-slice_fusion.2
  40.1 0.6 dynamic_slice.43
  41.5 1.4 constant_dynamic-slice_fusion.8
  43.0 1.3 constant_dynamic-slice_fusion.9
  44.4 3.6 %conditional.2 = (bf16[1,512,256]{2,1,0:T(8,128)(2,1)S(1)}) conditional(s32[]{:T(128)} %convert_element_type.105, (bf16[512,2,128]{2,0,1:T(8,128)(2,1)S(1)}, bf16[512,2,128]{2,0,1:T(8,128)(2,1)S(1)}, s32[]{:T(128)}, bf16[512,2,128]{2,0,1:T(8,128)(2,1)S(1)}, bf16[512,2,128]{2,0,1:T(8,128)(2,1)S(1)}, /*index=5*/bf16[256,256]{1,0:T(8,128)(2,1)S(1)}, ...), branch_computations={%region_3.3_spmd, %region_4.4_spmd} | conditional | flops 883687936 | bytes 18744356 | solution.py:84
  45.1 0.7 iota_compare_fusion.3
  46.2 0.3 fusion.12
  46.5 0.3 convolution_convert_fusion.1
  47.0 0.2 fusion.13
  47.5 0.2 convolution_add_fusion.3
  48.0 0.7 constant_dynamic-update-slice_fusion.2
  48.7 0.6 dynamic_slice.43
  50.1 1.4 constant_dynamic-slice_fusion.8
  51.5 1.3 constant_dynamic-slice_fusion.9
  53.0 3.6 %conditional.2 = (bf16[1,512,256]{2,1,0:T(8,128)(2,1)S(1)}) conditional(s32[]{:T(128)} %convert_element_type.105, (bf16[512,2,128]{2,0,1:T(8,128)(2,1)S(1)}, bf16[512,2,128]{2,0,1:T(8,128)(2,1)S(1)}, s32[]{:T(128)}, bf16[512,2,128]{2,0,1:T(8,128)(2,1)S(1)}, bf16[512,2,128]{2,0,1:T(8,128)(2,1)S(1)}, /*index=5*/bf16[256,256]{1,0:T(8,128)(2,1)S(1)}, ...), branch_computations={%region_3.3_spmd, %region_4.4_spmd} | conditional | flops 883687936 | bytes 18744356 | solution.py:84
  53.7 0.7 iota_compare_fusion.3
  54.7 0.3 fusion.12
  55.1 0.3 convolution_convert_fusion.1
  55.6 0.2 fusion.13
  56.1 0.2 convolution_add_fusion.3
  56.6 0.7 constant_dynamic-update-slice_fusion.2
  57.3 2.9 %gather_fusion.1 = bf16[16,128,256]{2,1,0:T(8,128)(2,1)} fusion(bf16[16,128,256]{2,1,0:T(8,128)(2,1)} %bitcast.104, s32[1024]{0:T(1024)S(1)} %pad_clamp_fusion), kind=kCustom, calls=%fused_computation.1 | custom fusion | bytes 2097216 | tf_op jit(solution)/shard_map/gather | solution.py:116
  60.2 5.1 %all-to-all-start.1 = ((bf16[16,128,256]{2,1,0:T(8,128)(2,1)}), bf16[16,128,256]{2,1,0:T(8,128)(2,1)}, u32[]{:S(2)}, u32[]{:S(2)}) async-start(bf16[16,128,256]{2,1,0:T(8,128)(2,1)} %gather_fusion.1), calls=%async_computation.1 | async-start | bytes 2097152 | tf_op jit(solution)/shard_map/all_to_all | solution.py:119
  65.3 25.3 %all-to-all-done.1 = bf16[16,128,256]{2,1,0:T(8,128)(2,1)} async-done(((bf16[16,128,256]{2,1,0:T(8,128)(2,1)}), bf16[16,128,256]{2,1,0:T(8,128)(2,1)}, u32[]{:S(2)}, u32[]{:S(2)}) %all-to-all-start.1) | async-done | bytes 1048608 | tf_op jit(solution)/shard_map/all_to_all | solution.py:119
  90.5 9.5 %while.22 = (s32[]{:T(128)}, f32[2048,256]{1,0:T(8,128)S(1)}, s32[4,512]{1,0:T(4,128)S(1)}, bf16[4,512,256]{2,1,0:T(8,128)(2,1)}, s32[]{:T(128)}, /*index=5*/s32[]{:T(128)}) while((s32[]{:T(128)}, f32[2048,256]{1,0:T(8,128)S(1)}, s32[4,512]{1,0:T(4,128)S(1)}, bf16[4,512,256]{2,1,0:T(8,128)(2,1)}, s32[]{:T(128)}, ...), condition=%wide.region_8.9_spmd.clone, body=%wide.region_7.8_spmd.clone.sunk | while | flops 538968064 | bytes 4462687 | solution.py:105
  90.5 2.3 %fusion.67 = f32[2048,256]{1,0:T(8,128)S(1)} fusion(f32[2048,256]{1,0:T(8,128)S(1)} %get-tuple-element.362, s32[512]{0:T(512)S(1)} %bitcast.106, pred[]{:T(512)S(6)} %compare.8, bf16[4,512,256]{2,1,0:T(8,128)(2,1)} %get-tuple-element.370, s32[]{:T(128)S(6)} %copy.74), kind=kOutput, calls=%fused_computation.60.clone.1 | convolution fusion | flops 538968064 | bytes 4458501 | tf_op jit(solution)/shard_map/while/body/eval_jaxpr/dot_general | solution.py:99
  92.9 2.3 %fusion.67 = f32[2048,256]{1,0:T(8,128)S(1)} fusion(f32[2048,256]{1,0:T(8,128)S(1)} %get-tuple-element.362, s32[512]{0:T(512)S(1)} %bitcast.106, pred[]{:T(512)S(6)} %compare.8, bf16[4,512,256]{2,1,0:T(8,128)(2,1)} %get-tuple-element.370, s32[]{:T(128)S(6)} %copy.74), kind=kOutput, calls=%fused_computation.60.clone.1 | convolution fusion | flops 538968064 | bytes 4458501 | tf_op jit(solution)/shard_map/while/body/eval_jaxpr/dot_general | solution.py:99
  95.3 2.3 %fusion.67 = f32[2048,256]{1,0:T(8,128)S(1)} fusion(f32[2048,256]{1,0:T(8,128)S(1)} %get-tuple-element.362, s32[512]{0:T(512)S(1)} %bitcast.106, pred[]{:T(512)S(6)} %compare.8, bf16[4,512,256]{2,1,0:T(8,128)(2,1)} %get-tuple-element.370, s32[]{:T(128)S(6)} %copy.74), kind=kOutput, calls=%fused_computation.60.clone.1 | convolution fusion | flops 538968064 | bytes 4458501 | tf_op jit(solution)/shard_map/while/body/eval_jaxpr/dot_general | solution.py:99
  97.7 2.3 %fusion.67 = f32[2048,256]{1,0:T(8,128)S(1)} fusion(f32[2048,256]{1,0:T(8,128)S(1)} %get-tuple-element.362, s32[512]{0:T(512)S(1)} %bitcast.106, pred[]{:T(512)S(6)} %compare.8, bf16[4,512,256]{2,1,0:T(8,128)(2,1)} %get-tuple-element.370, s32[]{:T(128)S(6)} %copy.74), kind=kOutput, calls=%fused_computation.60.clone.1 | convolution fusion | flops 538968064 | bytes 4458501 | tf_op jit(solution)/shard_map/while/body/eval_jaxpr/dot_general | solution.py:99
  100.0 1.3 copy-done.1
  101.4 0.6 convert_reduce_fusion
  102.0 45.7 %psum.7 = f32[]{:T(128)} all-reduce(f32[]{:T(128)} %convert_reduce_fusion), channel_id=1, replica_groups=mesh['group'=4,'batch'=8] {'group','batch'}, use_global_device_ids=true, to_apply=%region_1.0 | all-reduce | flops 1 | bytes 8 | tf_op jit(solution)/shard_map/psum | solution.py:110
  148.4 1.4 reduce-scatter.2.cloned.1.call-done
  149.8 1.7 %broadcast_multiply_fusion = f32[256,256]{1,0:T(8,128)} fusion(f32[256,256]{1,0:T(8,128)} %reduce-scatter.2.cloned.1.call-done, f32[]{:T(128)S(6)} %div.21), kind=kLoop, calls=%fused_computation.69 | loop fusion | flops 65536 | bytes 524292 | tf_op jit(solution)/shard_map/mul | solution.py:129
  (64 shorter events, 5.0 us)
Async XLA Ops:
  6.5 12.4 %copy-start = (bf16[2048,256]{1,0:T(8,128)(2,1)S(1)}, bf16[2048,256]{1,0:T(8,128)(2,1)}, u32[]{:S(2)}) copy-start(bf16[2048,256]{1,0:T(8,128)(2,1)} %param.14) | copy-start | bytes 3145732
  6.5 12.4 %copy-start.3 = (bf16[256,256]{1,0:T(8,128)(2,1)S(1)}, bf16[256,256]{1,0:T(8,128)(2,1)}, u32[]{:S(2)}) copy-start(bf16[256,256]{1,0:T(8,128)(2,1)} %param.16) | copy-start | bytes 393220
  10.4 49.8 %all-to-all-start = ((s32[4,4,128]{2,1,0:T(4,128)}), s32[4,4,128]{2,1,0:T(4,128)S(1)}, u32[]{:S(2)}, u32[]{:S(2)}) async-start(s32[4,4,128]{2,1,0:T(4,128)} %bitcast.20), calls=%async_computation | async-start | bytes 16384 | tf_op jit(solution)/shard_map/all_to_all | solution.py:120
  18.9 0.9 copy-start.4
  19.8 1.6 copy-start.2
  21.4 1.6 %copy-start.5 = (s32[4]{0:T(128)S(1)}, s32[4]{0:T(128)}, u32[]{:S(2)}) copy-start(s32[4]{0:T(128)} %param.19) | copy-start | bytes 52
  60.2 30.4 %all-to-all-start.1 = ((bf16[16,128,256]{2,1,0:T(8,128)(2,1)}), bf16[16,128,256]{2,1,0:T(8,128)(2,1)}, u32[]{:S(2)}, u32[]{:S(2)}) async-start(bf16[16,128,256]{2,1,0:T(8,128)(2,1)} %gather_fusion.1), calls=%async_computation.1 | async-start | bytes 2097152 | tf_op jit(solution)/shard_map/all_to_all | solution.py:119
  65.3 84.6 %reduce-scatter.2.cloned.1.call-start = ((), (), s32[]{:S(2)}) async-start(), calls=%async_computation.3 | async-start | bytes 2359296 | tf_op jit(solution)/shard_map/reduce_scatter | solution.py:123
  100.0 1.3 copy-start.1
Sparse Core Ops, SparseCore 0:
  101.5 48.2 reduce-scatter.1
where the time goes:
time: 159 us; the launch traced here: 158 us
  blocking collectives  45.7 us (29%)
  local copies, waits for them, and re-layouts  28 us (18%)
  waiting for transfers between devices  26.7 us (17%)
  matrix products  18.7 us (12%)
  between operations  14.1 us (9%)
  starting transfers between devices  11.4 us (7%)
  other arithmetic  7.41 us (5%)
  loops' own time  6.25 us (4%)
    psum x1, blocking collectives, on_device(): lax.psum(jnp.sum(lengths.astype(jnp.float32)), ('group', 'batch'))  45.7 us
    all_to_all x1, waiting for transfers between devices, on_device(): lax.all_to_all(tile_values, 'group', split_axis=0, concat_axis=0, tiled=T...  25.3 us
    dynamic_slice x28, local copies, waits for them, and re-layouts, token_grads(): result = lax.map(one_history, (query, key_rows, value, grad_heads, lengths))  14 us
    dot_general x4, matrix products, add_block(): jnp.dot(onehot, item[0], preferred_element_type=jnp.float32)  9.34 us
    all_to_all x1, starting transfers between devices, on_device(): lax.all_to_all(tile_rows, 'group', split_axis=0, concat_axis=0, tiled=True)  6.35 us
    all_to_all x1, starting transfers between devices, on_device(): lax.all_to_all(tile_values, 'group', split_axis=0, concat_axis=0, tiled=T...  5.09 us
    another operation x4, loops' own time, one_history(): return lax.cond(item[4] <= half_span, short_history, whole_history, item)  3.22 us
  transfers between devices with their start and end apart: 3, of which 2 were waited for; matrix products, arithmetic and copies ran while one was open for 24% of the time, Pallas kernels for 0%

commit v1 on v0

--- a/solution.py
+++ b/solution.py
@@ -1,13 +1,49 @@
+import functools
 import math
 import jax
 import jax.numpy as jnp
 from jax import lax
 from jax.sharding import PartitionSpec as P
+from jax.lax import axis_index, axis_size, ppermute
 
 HEADS = 2
 TILE = 128
 SEQ_LEN = 512
 ROWS_DEV = 256
+
+
+def _mix_shapes(local, row_dim, inner_x):
+    p_next = local.shape
+    u_next = local.reshape(
+        *p_next[:row_dim], inner_x, p_next[row_dim] // inner_x, *p_next[row_dim + 1 :]
+    )
+    formed = jnp.moveaxis(u_next, row_dim, 0)
+    return formed
+
+
+def produce_tracks(in_array, along_dim):
+    later = list(in_array.shape[1:])
+    later[along_dim] *= in_array.shape[0]
+    m_next = jnp.moveaxis(in_array, 0, along_dim).reshape(later)
+    return m_next
+
+
+def supply_widths(matrix, axis_id, local_block, w_in):
+    met_up = axis_size(axis_id)
+    block_next = axis_index(axis_id)
+    z, spare = (met_up, block_next)
+    x_now = _mix_shapes(matrix, local_block, z)
+    a_now = x_now
+    for h in range(1, z):
+        known, state_now = ((spare + h) % z, (spare - h) % z)
+        part_now = lax.dynamic_index_in_dim(x_now, known, 0)
+        t1 = ppermute(part_now, axis_id, [(k, (k + h) % z) for k in range(z)])
+        a_now = lax.dynamic_update_slice_in_dim(a_now, t1, state_now, axis=0)
+    field_out = produce_tracks(a_now, w_in)
+    return field_out
+
+
+put_table = functools.partial(supply_widths, axis_id="group", local_block=0, w_in=0)
 
 
 def sequence_grads(query, key_rows, value, grad_out, count, w_query, w_key, w_value):
@@ -116,7 +152,7 @@
     tile_values = token_grad.reshape(-1, TILE, width)[ranking]
     tile_rows = item_rows.reshape(-1, TILE)[ranking]
     got_values, got_rows = (
-        lax.all_to_all(tile_values, "group", split_axis=0, concat_axis=0, tiled=True),
+        put_table(tile_values),
         lax.all_to_all(tile_rows, "group", split_axis=0, concat_axis=0, tiled=True),
     )
     empty_rows = jnp.zeros((ROWS_DEV * lax.axis_size("batch"), width), jnp.float32)

time: 159 us -> 154 us (0.969)
  waiting for transfers between devices: 26.7 us -> 21.1 us
  starting transfers between devices: 11.4 us -> 8.76 us
  local copies, waits for them, and re-layouts: 28 us -> 30 us
  blocking collectives: 45.7 us -> 47.6 us
    all_to_all x1 -> x0, waiting for transfers between devices: 25.3 us -> none  [on_device(): lax.all_to_all(tile_values, 'group', split_axis=0, concat_axis=0, tiled=T...]
    all_to_all x1, waiting for transfers between devices: 0.01 us -> 12.1 us  [on_device(): lax.all_to_all(tile_rows, 'group', split_axis=0, concat_axis=0, tiled=True)]
    ppermute x0 -> x3, waiting for transfers between devices: none -> 8.32 us  [supply_widths(): t1 = ppermute(part_now, axis_id, [(k, (k + h) % z) for k in range(z)])]
    ppermute x0 -> x3, starting transfers between devices: none -> 5.19 us  [supply_widths(): t1 = ppermute(part_now, axis_id, [(k, (k + h) % z) for k in range(z)])]
    all_to_all x1 -> x0, starting transfers between devices: 5.09 us -> none  [on_device(): lax.all_to_all(tile_values, 'group', split_axis=0, concat_axis=0, tiled=T...]
    dynamic_update_slice x0 -> x2, local copies, waits for them, and re-layouts: none -> 3.33 us  [supply_widths(): a_now = lax.dynamic_update_slice_in_dim(a_now, t1, state_now, axis=0)]
    all_to_all x1, starting transfers between devices: 6.35 us -> 3.57 us  [on_device(): lax.all_to_all(tile_rows, 'group', split_axis=0, concat_axis=0, tiled=True)]
    psum x1, blocking collectives: 45.7 us -> 47.6 us  [on_device(): lax.psum(jnp.sum(lengths.astype(jnp.float32)), ('group', 'batch'))]
  transfers between devices with their start and end apart: 3 -> 5, of which waited for: 2 -> 3; matrix products, arithmetic and copies ran while one was open for 24% -> 2% of each run, Pallas kernels for 0% -> 0%
where the time goes in v1:
time: 154 us
  blocking collectives  47.6 us (31%)
  local copies, waits for them, and re-layouts  30 us (19%)
  waiting for transfers between devices  21.1 us (14%)
  matrix products  18.6 us (12%)
  between operations  14.2 us (9%)
  starting transfers between devices  8.76 us (6%)
  other arithmetic  7.28 us (5%)
  loops' own time  6.01 us (4%)
    psum x1, blocking collectives, on_device(): lax.psum(jnp.sum(lengths.astype(jnp.float32)), ('group', 'batch'))  47.6 us
    dynamic_slice x28, local copies, waits for them, and re-layouts, token_grads(): result = lax.map(one_history, (query, key_rows, value, grad_heads, lengths))  13.8 us
    all_to_all x1, waiting for transfers between devices, on_device(): lax.all_to_all(tile_rows, 'group', split_axis=0, concat_axis=0, tiled=True)  12.1 us
    dot_general x4, matrix products, add_block(): jnp.dot(onehot, item[0], preferred_element_type=jnp.float32)  9.34 us
    ppermute x3, waiting for transfers between devices, supply_widths(): t1 = ppermute(part_now, axis_id, [(k, (k + h) % z) for k in range(z)])  8.32 us
    ppermute x3, starting transfers between devices, supply_widths(): t1 = ppermute(part_now, axis_id, [(k, (k + h) % z) for k in range(z)])  5.19 us
    all_to_all x1, starting transfers between devices, on_device(): lax.all_to_all(tile_rows, 'group', split_axis=0, concat_axis=0, tiled=True)  3.57 us
    reshape x3, local copies, waits for them, and re-layouts, project(): return jnp.dot(embeds, weight_matrix, preferred_element_type=jnp.float32)...  3.42 us
  transfers between devices with their start and end apart: 5, of which 3 were waited for; matrix products, arithmetic and copies ran while one was open for 2% of the time, Pallas kernels for 0%

profile of v1, /device:TPU:0, one launch (start us, length us, event | category | flops | bytes accessed | tf_op | source)
XLA Modules:
  0.0 153.6 jit_solution(10721177313169218433)
XLA Ops:
  6.5 2.0 %sort.17 = (s32[16]{0:T(128)}, s32[16]{0:T(128)S(1)}) sort(s32[16]{0:T(128)} %param.21, s32[16]{0:T(128)S(1)} %iota.48), dimensions={0}, to_apply=%region_6.7 | sort | flops 64 | bytes 256 | tf_op jit(solution)/shard_map/jit(argsort)/sort | solution.py:151
  8.5 1.3 reshape.82
  9.9 0.4 convolution_convert_fusion.4
  10.4 1.1 reshape.80
  11.5 0.4 convolution_convert_fusion.3
  11.9 1.2 reshape.81
  13.1 0.4 convolution_convert_fusion.2
  13.5 1.1 reshape.83
  14.7 33.6 %while.21 = (s32[]{:T(128)}, bf16[4,512,256]{2,1,0:T(8,128)(2,1)}, s32[4]{0:T(128)S(1)}, bf16[4,512,2,128]{3,2,1,0:T(2,128)(2,1)}, bf16[4,512,2,128]{3,2,1,0:T(2...) while((s32[]{:T(128)}, bf16[4,512,256]{2,1,0:T(8,128)(2,1)}, ...), condition=%wide.region_5.6_spmd, body=%wide.region_2.5_spmd.sunk | while | flops 883687936 | bytes 23463240 | solution.py:122
  14.7 0.6 dynamic_slice.59
  15.9 1.3 constant_dynamic-slice_fusion.11
  17.3 1.4 constant_dynamic-slice_fusion.12
  18.8 3.5 %conditional.2 = (bf16[1,512,256]{2,1,0:T(8,128)(2,1)S(1)}) conditional(s32[]{:T(128)} %convert_element_type.105, (bf16[512,2,128]{2,0,1:T(8,128)(2,1)S(1)}, bf16[512,2,128]{2,0,1:T(8,128)(2,1)S(1)}, s32[]{:T(128)}, bf16[512,2,128]{2,0,1:T(8,128)(2,1)S(1)}, bf16[512,2,128]{2,0,1:T(8,128)(2,1)S(1)}, /*index=5*/bf16[256,256]{1,0:T(8,128)(2,1)S(1)}, ...), branch_computations={%region_3.3_spmd, %region_4.4_spmd} | conditional | flops 883687936 | bytes 18744356 | solution.py:120
  19.5 0.7 iota_compare_fusion.3
  20.5 0.3 fusion.12
  20.8 0.3 convolution_convert_fusion.1
  21.4 0.2 fusion.13
  22.4 0.7 constant_dynamic-update-slice_fusion.5
  23.1 0.6 dynamic_slice.59
  24.3 1.3 constant_dynamic-slice_fusion.11
  25.7 1.4 constant_dynamic-slice_fusion.12
  27.2 3.5 %conditional.2 = (bf16[1,512,256]{2,1,0:T(8,128)(2,1)S(1)}) conditional(s32[]{:T(128)} %convert_element_type.105, (bf16[512,2,128]{2,0,1:T(8,128)(2,1)S(1)}, bf16[512,2,128]{2,0,1:T(8,128)(2,1)S(1)}, s32[]{:T(128)}, bf16[512,2,128]{2,0,1:T(8,128)(2,1)S(1)}, bf16[512,2,128]{2,0,1:T(8,128)(2,1)S(1)}, /*index=5*/bf16[256,256]{1,0:T(8,128)(2,1)S(1)}, ...), branch_computations={%region_3.3_spmd, %region_4.4_spmd} | conditional | flops 883687936 | bytes 18744356 | solution.py:120
  27.9 0.7 iota_compare_fusion.3
  28.9 0.3 fusion.12
  29.3 0.3 convolution_convert_fusion.1
  29.8 0.2 fusion.13
  30.8 0.7 constant_dynamic-update-slice_fusion.5
  31.5 0.6 dynamic_slice.59
  32.7 1.3 constant_dynamic-slice_fusion.11
  34.1 1.4 constant_dynamic-slice_fusion.12
  35.6 3.5 %conditional.2 = (bf16[1,512,256]{2,1,0:T(8,128)(2,1)S(1)}) conditional(s32[]{:T(128)} %convert_element_type.105, (bf16[512,2,128]{2,0,1:T(8,128)(2,1)S(1)}, bf16[512,2,128]{2,0,1:T(8,128)(2,1)S(1)}, s32[]{:T(128)}, bf16[512,2,128]{2,0,1:T(8,128)(2,1)S(1)}, bf16[512,2,128]{2,0,1:T(8,128)(2,1)S(1)}, /*index=5*/bf16[256,256]{1,0:T(8,128)(2,1)S(1)}, ...), branch_computations={%region_3.3_spmd, %region_4.4_spmd} | conditional | flops 883687936 | bytes 18744356 | solution.py:120
  36.3 0.7 iota_compare_fusion.3
  37.3 0.3 fusion.12
  37.7 0.3 convolution_convert_fusion.1
  39.2 0.7 constant_dynamic-update-slice_fusion.5
  39.9 0.6 dynamic_slice.59
  41.1 1.3 constant_dynamic-slice_fusion.11
  42.5 1.4 constant_dynamic-slice_fusion.12
  44.0 3.5 %conditional.2 = (bf16[1,512,256]{2,1,0:T(8,128)(2,1)S(1)}) conditional(s32[]{:T(128)} %convert_element_type.105, (bf16[512,2,128]{2,0,1:T(8,128)(2,1)S(1)}, bf16[512,2,128]{2,0,1:T(8,128)(2,1)S(1)}, s32[]{:T(128)}, bf16[512,2,128]{2,0,1:T(8,128)(2,1)S(1)}, bf16[512,2,128]{2,0,1:T(8,128)(2,1)S(1)}, /*index=5*/bf16[256,256]{1,0:T(8,128)(2,1)S(1)}, ...), branch_computations={%region_3.3_spmd, %region_4.4_spmd} | conditional | flops 883687936 | bytes 18744356 | solution.py:120
  44.7 0.7 iota_compare_fusion.3
  45.7 0.3 fusion.12
  46.1 0.3 convolution_convert_fusion.1
  47.6 0.7 constant_dynamic-update-slice_fusion.5
  48.3 1.9 %gather_fusion.1 = bf16[16,128,256]{2,1,0:T(8,128)(2,1)S(1)} fusion(bf16[16,128,256]{2,1,0:T(8,128)(2,1)} %bitcast.108, s32[1024]{0:T(1024)S(1)} %pad_clamp_fusion), kind=kCustom, calls=%fused_computation.1 | custom fusion | bytes 2097216 | tf_op jit(solution)/shard_map/gather | solution.py:152
  50.2 3.1 %collective-permute-start = (bf16[1,4,128,256]{3,2,1,0:T(8,128)(2,1)S(1)}, bf16[1,4,128,256]{3,2,1,0:T(8,128)(2,1)S(1)}, u32[]{:S(2)}, u32[]{:S(2)}) collective-permute-start(bf16[1,4,128,256]{3,2,1,0:T(8,128)(2,1)S(1)} %constant_dynamic-slice_fusion.7), channel_id=1, source_target_pairs={{0,8},{8,16},{16,24},{24,0},{1,9},{9,17},{17,25},{25,1},{2,10},{10... | collective-permute-start | bytes 786440 | tf_op jit(solution)/shard_map/ppermute | solution.py:40
  53.3 8.3 %collective-permute-done = bf16[1,4,128,256]{3,2,1,0:T(8,128)(2,1)S(1)} collective-permute-done((bf16[1,4,128,256]{3,2,1,0:T(8,128)(2,1)S(1)}, bf16[1,4,128,256]{3,2,1,0:T(8,128)(2,1)S(1)}, u32[]{:S(2)}, u32[]{:S(2)}) %collective-permute-start) | collective-permute-done | bytes 262176 | tf_op jit(solution)/shard_map/ppermute | solution.py:40
  61.6 0.8 constant_dynamic-slice_fusion.5
  62.4 0.7 collective-permute-start.1
  63.1 1.4 collective-permute-start.2
  64.5 1.1 gather_fusion
  65.6 3.6 %all-to-all-start = ((s32[4,4,128]{2,1,0:T(4,128)}), s32[4,4,128]{2,1,0:T(4,128)S(1)}, u32[]{:S(2)}, u32[]{:S(2)}) async-start(s32[4,4,128]{2,1,0:T(4,128)} %bitcast.20), calls=%async_computation | async-start | bytes 16384 | tf_op jit(solution)/shard_map/all_to_all | solution.py:156
  69.2 12.1 %all-to-all-done = s32[4,4,128]{2,1,0:T(4,128)S(1)} async-done(((s32[4,4,128]{2,1,0:T(4,128)}), s32[4,4,128]{2,1,0:T(4,128)S(1)}, u32[]{:S(2)}, u32[]{:S(2)}) %all-to-all-start) | async-done | bytes 8224 | tf_op jit(solution)/shard_map/all_to_all | solution.py:156
  81.3 1.7 %constant_dynamic-update-slice_fusion.2 = bf16[4,4,128,256]{3,2,1,0:T(8,128)(2,1)} fusion(bf16[4,4,128,256]{3,2,1,0:T(8,128)(2,1)} %copy-done.5, bf16[1,4,128,256]{3,2,1,0:T(8,128)(2,1)} %collective-permute-done.1, s32[]{:T(128)S(6)} %select_n.58), kind=kLoop, calls=%fused_computation.75 | loop fusion | bytes 524292 | tf_op jit(solution)/shard_map/dynamic_update_slice | solution.py:41
  83.0 1.7 %constant_dynamic-update-slice_fusion.1 = bf16[4,4,128,256]{3,2,1,0:T(8,128)(2,1)} fusion(bf16[4,4,128,256]{3,2,1,0:T(8,128)(2,1)} %constant_dynamic-update-slice_fusion.2, bf16[1,4,128,256]{3,2,1,0:T(8,128)(2,1)} %collective-permute-done.2, s32[]{:T(128)S(6)} %select_n.62), kind=kLoop, calls=%fused_computation.73 | loop fusion | bytes 524292 | tf_op jit(solution)/shard_map/dynamic_update_slice | solution.py:41
  84.6 9.5 %while.22 = (s32[]{:T(128)}, f32[2048,256]{1,0:T(8,128)S(1)}, s32[4,512]{1,0:T(4,128)S(1)}, bf16[4,512,256]{2,1,0:T(8,128)(2,1)}, s32[]{:T(128)}, /*index=5*/s32[]{:T(128)}) while((s32[]{:T(128)}, f32[2048,256]{1,0:T(8,128)S(1)}, s32[4,512]{1,0:T(4,128)S(1)}, bf16[4,512,256]{2,1,0:T(8,128)(2,1)}, s32[]{:T(128)}, ...), condition=%wide.region_8.9_spmd.clone, body=%wide.region_7.8_spmd.clone.sunk | while | flops 538968064 | bytes 4462687 | solution.py:141
  84.6 2.3 %fusion.67 = f32[2048,256]{1,0:T(8,128)S(1)} fusion(f32[2048,256]{1,0:T(8,128)S(1)} %get-tuple-element.365, s32[512]{0:T(512)S(1)} %bitcast.110, pred[]{:T(512)S(6)} %compare.14, bf16[4,512,256]{2,1,0:T(8,128)(2,1)} %get-tuple-element.373, s32[]{:T(128)S(6)} %copy.77), kind=kOutput, calls=%fused_computation.60.clone.1 | convolution fusion | flops 538968064 | bytes 4458501 | tf_op jit(solution)/shard_map/while/body/eval_jaxpr/dot_general | solution.py:135
  87.0 2.3 %fusion.67 = f32[2048,256]{1,0:T(8,128)S(1)} fusion(f32[2048,256]{1,0:T(8,128)S(1)} %get-tuple-element.365, s32[512]{0:T(512)S(1)} %bitcast.110, pred[]{:T(512)S(6)} %compare.14, bf16[4,512,256]{2,1,0:T(8,128)(2,1)} %get-tuple-element.373, s32[]{:T(128)S(6)} %copy.77), kind=kOutput, calls=%fused_computation.60.clone.1 | convolution fusion | flops 538968064 | bytes 4458501 | tf_op jit(solution)/shard_map/while/body/eval_jaxpr/dot_general | solution.py:135
  89.4 2.3 %fusion.67 = f32[2048,256]{1,0:T(8,128)S(1)} fusion(f32[2048,256]{1,0:T(8,128)S(1)} %get-tuple-element.365, s32[512]{0:T(512)S(1)} %bitcast.110, pred[]{:T(512)S(6)} %compare.14, bf16[4,512,256]{2,1,0:T(8,128)(2,1)} %get-tuple-element.373, s32[]{:T(128)S(6)} %copy.77), kind=kOutput, calls=%fused_computation.60.clone.1 | convolution fusion | flops 538968064 | bytes 4458501 | tf_op jit(solution)/shard_map/while/body/eval_jaxpr/dot_general | solution.py:135
  91.7 2.3 %fusion.67 = f32[2048,256]{1,0:T(8,128)S(1)} fusion(f32[2048,256]{1,0:T(8,128)S(1)} %get-tuple-element.365, s32[512]{0:T(512)S(1)} %bitcast.110, pred[]{:T(512)S(6)} %compare.14, bf16[4,512,256]{2,1,0:T(8,128)(2,1)} %get-tuple-element.373, s32[]{:T(128)S(6)} %copy.77), kind=kOutput, calls=%fused_computation.60.clone.1 | convolution fusion | flops 538968064 | bytes 4458501 | tf_op jit(solution)/shard_map/while/body/eval_jaxpr/dot_general | solution.py:135
  94.1 1.3 copy-done.1
  95.5 0.6 convert_reduce_fusion
  96.1 47.6 %psum.7 = f32[]{:T(128)} all-reduce(f32[]{:T(128)} %convert_reduce_fusion), channel_id=1, replica_groups=mesh['group'=4,'batch'=8] {'group','batch'}, use_global_device_ids=true, to_apply=%region_1.0 | all-reduce | flops 1 | bytes 8 | tf_op jit(solution)/shard_map/psum | solution.py:146
  144.4 0.6 reduce-scatter.2.cloned.1.call-done
  145.0 1.7 %broadcast_multiply_fusion = f32[256,256]{1,0:T(8,128)} fusion(f32[256,256]{1,0:T(8,128)} %reduce-scatter.2.cloned.1.call-done, f32[]{:T(128)S(6)} %div.21), kind=kLoop, calls=%fused_computation.69 | loop fusion | flops 65536 | bytes 524292 | tf_op jit(solution)/shard_map/mul | solution.py:165
  (76 shorter events, 6.2 us)
Async XLA Ops:
  6.5 3.4 %copy-start = (bf16[2048,256]{1,0:T(8,128)(2,1)S(1)}, bf16[2048,256]{1,0:T(8,128)(2,1)}, u32[]{:S(2)}) copy-start(bf16[2048,256]{1,0:T(8,128)(2,1)} %param.14) | copy-start | bytes 3145732
  6.5 3.4 %copy-start.3 = (bf16[256,256]{1,0:T(8,128)(2,1)S(1)}, bf16[256,256]{1,0:T(8,128)(2,1)}, u32[]{:S(2)}) copy-start(bf16[256,256]{1,0:T(8,128)(2,1)} %param.16) | copy-start | bytes 393220
  9.9 1.6 %copy-start.4 = (bf16[256,256]{1,0:T(8,128)(2,1)S(1)}, bf16[256,256]{1,0:T(8,128)(2,1)}, u32[]{:S(2)}) copy-start(bf16[256,256]{1,0:T(8,128)(2,1)} %param.17) | copy-start | bytes 393220
  11.5 1.6 %copy-start.2 = (bf16[256,256]{1,0:T(8,128)(2,1)S(1)}, bf16[256,256]{1,0:T(8,128)(2,1)}, u32[]{:S(2)}) copy-start(bf16[256,256]{1,0:T(8,128)(2,1)} %param.18) | copy-start | bytes 393220
  13.1 1.6 %copy-start.7 = (s32[4]{0:T(128)S(1)}, s32[4]{0:T(128)}, u32[]{:S(2)}) copy-start(s32[4]{0:T(128)} %param.19) | copy-start | bytes 52
  48.3 16.2 %copy-start.6 = (s32[2048]{0:T(1024)S(1)}, s32[2048]{0:T(1024)}, u32[]{:S(2)}) copy-start(s32[2048]{0:T(1024)} %param.20) | copy-start | bytes 24580
  50.2 11.4 %collective-permute-start = (bf16[1,4,128,256]{3,2,1,0:T(8,128)(2,1)S(1)}, bf16[1,4,128,256]{3,2,1,0:T(8,128)(2,1)S(1)}, u32[]{:S(2)}, u32[]{:S(2)}) collective-permute-start(bf16[1,4,128,256]{3,2,1,0:T(8,128)(2,1)S(1)} %constant_dynamic-slice_fusion.7), channel_id=1, source_target_pairs={{0,8},{8,16},{16,24},{24,0},{1,9},{9,17},{17,25},{25,1},{2,10},{10... | collective-permute-start | bytes 786440 | tf_op jit(solution)/shard_map/ppermute | solution.py:40
  62.4 6.8 %copy-start.5 = (bf16[4,4,128,256]{3,2,1,0:T(8,128)(2,1)}, bf16[4,4,128,256]{3,2,1,0:T(8,128)(2,1)S(1)}, u32[]{:S(2)}) copy-start(bf16[4,4,128,256]{3,2,1,0:T(8,128)(2,1)S(1)} %get-tuple-element.227) | copy-start | bytes 3145732
  62.4 18.9 %collective-permute-start.1 = (bf16[1,4,128,256]{3,2,1,0:T(8,128)(2,1)}, bf16[1,4,128,256]{3,2,1,0:T(8,128)(2,1)}, u32[]{:S(2)}, u32[]{:S(2)}) collective-permute-start(bf16[1,4,128,256]{3,2,1,0:T(8,128)(2,1)} %get-tuple-element.226), channel_id=1, source_target_pairs={{0,16},{8,24},{16,0},{24,8},{1,17},{9,25},{17,1},{25,9},{2,18},{10... | collective-permute-start | bytes 786440 | tf_op jit(solution)/shard_map/ppermute | solution.py:40
  63.1 19.9 %collective-permute-start.2 = (bf16[1,4,128,256]{3,2,1,0:T(8,128)(2,1)S(1)}, bf16[1,4,128,256]{3,2,1,0:T(8,128)(2,1)}, u32[]{:S(2)}, u32[]{:S(2)}) collective-permute-start(bf16[1,4,128,256]{3,2,1,0:T(8,128)(2,1)S(1)} %get-tuple-element.225), channel_id=1, source_target_pairs={{0,24},{8,0},{16,8},{24,16},{1,25},{9,1},{17,9},{25,17},{2,26},{10... | collective-permute-start | bytes 786440 | tf_op jit(solution)/shard_map/ppermute | solution.py:40
  65.6 15.7 %all-to-all-start = ((s32[4,4,128]{2,1,0:T(4,128)}), s32[4,4,128]{2,1,0:T(4,128)S(1)}, u32[]{:S(2)}, u32[]{:S(2)}) async-start(s32[4,4,128]{2,1,0:T(4,128)} %bitcast.20), calls=%async_computation | async-start | bytes 16384 | tf_op jit(solution)/shard_map/all_to_all | solution.py:156
  69.2 75.9 %reduce-scatter.2.cloned.1.call-start = ((), (), s32[]{:S(2)}) async-start(), calls=%async_computation.2 | async-start | bytes 2359296 | tf_op jit(solution)/shard_map/reduce_scatter | solution.py:159
  94.1 1.3 copy-start.1
Sparse Core Ops, SparseCore 0:
  95.6 49.3 reduce-scatter.1
